TPU v7x, 16 devices: a 4x2x1 block of a 4x4x8 slice. The times are simulated.
16 devices in a mesh: dp: 2 (over y, z), tp: 8 (over x, core).
Axes of the slice: x: 4, y: 2, z: 1, core: 2. Of those that a mesh axis runs over, the one named last changes fastest.
The devices are a block of a 4x4x8 slice.
Arguments:
- hidden_in: bfloat16 [256, 5120], P(('dp', 'tp')), parts along dimension 0
- attn_norm: bfloat16 [5120], replicated
- mlp_norm: bfloat16 [5120], replicated
- w_query: bfloat16 [5120, 40, 128], P(None, 'tp')
- w_key: bfloat16 [5120, 8, 128], replicated
- w_value: bfloat16 [5120, 8, 128], replicated
- w_out: bfloat16 [40, 128, 5120], P('tp')
- w_gate: bfloat16 [5120, 17408], P(None, 'tp')
- w_up: bfloat16 [5120, 17408], P(None, 'tp')
- w_down: bfloat16 [17408, 5120], P('tp')
Outputs:
- output 1: bfloat16 [256, 5120], P(('dp', 'tp')), parts along dimension 0
- output 2: bfloat16 [256, 8, 128], P('dp', 'tp'), parts along dimension 0
- output 3: bfloat16 [256, 8, 128], P('dp', 'tp'), parts along dimension 0
There are 2 independent parts. A program takes and returns all parts, laid end to end along the dimension named above; an argument that names none is the same for every part.
All inputs are finite; a program needn't handle non-finite values.
Results may differ from a plain program's by a relative error of at most 0.0170683.
Values are sent between devices in bfloat16 or wider.
A program may use at most 768 MiB of HBM per device.

v0:
```python
import jax
import jax.numpy as jnp
from jax import lax
from jax.sharding import PartitionSpec as P


def rms_norm(rows_in, gain_vec):
    rows_f = rows_in.astype(jnp.float32)
    mean_sq = jnp.mean(rows_f * rows_f, axis=-1, keepdims=True)
    return (rows_f * lax.rsqrt(mean_sq + 1e-5) * gain_vec.astype(jnp.float32)).astype(jnp.bfloat16)


def apply_rope(heads_f, positions):
    head_dim = heads_f.shape[-1]
    half_dim = head_dim // 2
    inv_freq = 1.0 / (500000.0 ** (jnp.arange(half_dim).astype(jnp.float32) * (2.0 / head_dim)))
    angles = positions[:, None] * inv_freq[None, :]
    cosine = jnp.cos(angles)[:, None, :]
    sine_val = jnp.sin(angles)[:, None, :]
    first_half = heads_f[..., :half_dim]
    second_half = heads_f[..., half_dim:]
    return jnp.concatenate([first_half * cosine - second_half * sine_val, second_half * cosine + first_half * sine_val], axis=-1)


def causal_attention(q_rot, k_rot, v_local):
    tokens = q_rot.shape[0]
    head_dim = q_rot.shape[-1]
    n_split = 8
    block_len = tokens // n_split
    pieces = []
    for block_idx in range(n_split):
        key_stop = (block_idx + 1) * block_len
        q_block = q_rot[block_idx * block_len:key_stop]
        scores = jnp.einsum("qgrd,kgd->grqk", q_block, k_rot[:key_stop], preferred_element_type=jnp.float32) * (head_dim ** -0.5)
        query_pos = block_idx * block_len + jnp.arange(block_len)
        visible = jnp.arange(key_stop)[None, :] <= query_pos[:, None]
        scores = jnp.where(visible, scores, -1e30)
        probs_bf = jax.nn.softmax(scores, axis=-1).astype(jnp.bfloat16)
        block_out = jnp.einsum("grqk,kgd->qgrd", probs_bf, v_local[:key_stop], preferred_element_type=jnp.float32)
        pieces.append(block_out.astype(jnp.bfloat16))
    return jnp.concatenate(pieces, axis=0)


def solution(mesh):
    tp_size = mesh.shape["tp"]

    def local_layer(hidden_in, attn_norm, mlp_norm, w_query, w_key, w_value, w_out, w_gate, w_up, w_down):
        kv_heads = w_key.shape[1]
        local_heads = w_query.shape[1]
        head_dim = w_query.shape[2]
        kv_local = max(kv_heads // tp_size, 1)
        first_kv = (lax.axis_index("tp") * kv_heads) // tp_size
        key_local = lax.dynamic_slice_in_dim(w_key, first_kv, kv_local, axis=1)
        value_local = lax.dynamic_slice_in_dim(w_value, first_kv, kv_local, axis=1)
        normed = rms_norm(hidden_in, attn_norm)
        gathered = lax.all_gather(normed, "tp", axis=0, tiled=True)
        tokens = gathered.shape[0]
        positions = jnp.arange(tokens).astype(jnp.float32)
        q_proj = jnp.einsum("td,dhe->the", gathered, w_query, preferred_element_type=jnp.float32)
        k_proj = jnp.einsum("td,dge->tge", gathered, key_local, preferred_element_type=jnp.float32)
        v_local = jnp.einsum("td,dge->tge", gathered, value_local, preferred_element_type=jnp.float32).astype(jnp.bfloat16)
        q_rot = apply_rope(q_proj, positions).astype(jnp.bfloat16).reshape(tokens, kv_local, local_heads // kv_local, head_dim)
        k_rot = apply_rope(k_proj, positions).astype(jnp.bfloat16)
        attn_out = causal_attention(q_rot, k_rot, v_local).reshape(tokens, local_heads, head_dim)
        attn_part = jnp.einsum("the,hed->td", attn_out, w_out, preferred_element_type=jnp.float32).astype(jnp.bfloat16)
        attn_sum = lax.psum_scatter(attn_part, "tp", scatter_dimension=0, tiled=True)
        resid_mid = (hidden_in.astype(jnp.float32) + attn_sum.astype(jnp.float32)).astype(jnp.bfloat16)
        normed_mlp = rms_norm(resid_mid, mlp_norm)
        gathered_mlp = lax.all_gather(normed_mlp, "tp", axis=0, tiled=True)
        gate_proj = jnp.dot(gathered_mlp, w_gate, preferred_element_type=jnp.float32)
        up_proj = jnp.dot(gathered_mlp, w_up, preferred_element_type=jnp.float32)
        mlp_act = (jax.nn.silu(gate_proj) * up_proj).astype(jnp.bfloat16)
        mlp_part = jnp.dot(mlp_act, w_down, preferred_element_type=jnp.float32).astype(jnp.bfloat16)
        mlp_sum = lax.psum_scatter(mlp_part, "tp", scatter_dimension=0, tiled=True)
        hidden_out = (resid_mid.astype(jnp.float32) + mlp_sum.astype(jnp.float32)).astype(jnp.bfloat16)
        return hidden_out, k_rot, v_local

    row_spec = P(("dp", "tp"), None)
    cache_spec = P("dp", "tp", None)
    return jax.shard_map(local_layer, mesh=mesh, in_specs=(row_spec, P(), P(), P(None, "tp", None), P(), P(), P("tp", None, None), P(None, "tp"), P(None, "tp"), P("tp", None)), out_specs=(row_spec, cache_spec, cache_spec), check_vma=False)
```

profile of v0, /device:TPU:113, one launch (start us, length us, event | category | flops | bytes accessed | tf_op | source)
XLA Modules:
  0.0 168.1 jit_solution(16079035664549557409)
XLA Ops:
  7.2 0.7 convert_element_type.198
  8.0 1.1 fusion.38
  9.0 1.7 %fusion.40 = bf16[16,5120]{1,0:T(8,128)(2,1)} fusion(bf16[16,5120]{1,0:T(8,128)(2,1)} %param.10, f32[5120]{0:T(1024)S(1)} %convert_element_type.198, f32[16]{0:T(128)S(1)} %add_rsqrt_fusion.1), kind=kLoop, calls=%fused_computation.67 | loop fusion | flops 327680 | bytes 348224 | tf_op jit(solution)/shard_map/convert_element_type | solution.py:10
  11.0 9.6 %copy.34 = bf16[5120,5,128]{0,2,1:T(8,128)(2,1)} copy(bf16[5120,5,128]{2,0,1:T(8,128)(2,1)} %param.13) | data formatting | bytes 13107200 | tf_op args[3]
  20.6 0.1 iota_compare_fusion.6
  20.6 0.1 iota_compare_fusion.5
  21.1 0.2 multiply_cosine_fusion
  21.3 11.6 %constant_dynamic-slice_fusion = (bf16[5120,1,128]{2,1,0:T(2,128)(2,1)S(1)}, bf16[5120,1,128]{2,1,0:T(2,128)(2,1)}) fusion(bf16[5120,8,128]{2,1,0:T(8,128)(2,1)} %param.14, s32[]{:T(128)S(6)} %select_n.42, bf16[5120,8,128]{2,1,0:T(8,128)(2,1)} %param.15), kind=kLoop, calls=%fused_computation.209 | loop fusion | bytes 5242884 | tf_op jit(solution)/shard_map/dynamic_slice | solution.py:53
  32.8 0.9 all-gather.3.cloned.1.call-done
  33.8 2.0 %fusion.4 = f32[128,1,128]{0,2,1:T(8,128)S(1)} fusion(bf16[128,5120]{1,0:T(8,128)(2,1)} %all-gather.3.cloned.1.call-done, bf16[5120,1,128]{2,1,0:T(2,128)(2,1)S(1)} %get-tuple-element.31), kind=kOutput, calls=%fused_computation.9 | convolution fusion | flops 167772160 | bytes 2686976 | tf_op jit(solution)/shard_map/td,dge->tge/dot_general | solution.py:60
  35.8 0.2 fusion.77
  36.1 4.9 %fusion.134 = f32[128,640]{0,1:S(1)} fusion(bf16[128,5120]{1,0:T(8,128)(2,1)S(1)} %copy-done, bf16[5120,640]{0,1:T(8,128)(2,1)} %bitcast.241), kind=kOutput, calls=%fused_computation.228 | convolution fusion | flops 838860800 | bytes 8192000
  41.0 0.2 fusion.126
  41.2 0.3 fusion.127
  41.5 0.4 fusion.128
  41.9 0.4 fusion.129
  42.3 0.4 fusion.130
  42.7 0.4 fusion.131
  43.1 0.4 fusion.132
  43.5 0.5 fusion.5
  44.1 0.2 fusion.23
  44.3 0.2 fusion.67
  44.4 0.2 fusion.25
  44.7 0.2 fusion.68
  44.8 0.2 fusion.27
  45.1 0.2 fusion.69
  45.2 0.2 fusion.29
  45.4 0.2 fusion.70
  45.6 0.2 fusion.31
  45.8 0.2 fusion.71
  46.0 0.2 fusion.33
  46.2 0.2 fusion.72
  46.4 0.2 fusion.35
  46.6 0.3 fusion.133
  46.9 0.2 fusion.73
  47.1 0.2 fusion.37
  47.4 2.3 %fusion = bf16[128,5120]{1,0:T(8,128)(2,1)} fusion(bf16[5,128,5120]{2,1,0:T(8,128)(2,1)S(1)} %bitcast.243, bf16[128,1,5,128]{3,0,2,1:T(8,128)(2,1)S(1)} %fusion.37), kind=kOutput, calls=%fused_computation.1 | convolution fusion | flops 839516160 | bytes 8028160 | tf_op jit(solution)/shard_map/the,hed->td/dot_general | solution.py:65
  49.8 0.6 copy-done.5
  50.4 27.0 %reduce-scatter.3.cloned.1.call-done = bf16[16,5120]{1,0:T(8,128)(2,1)} async-done(((bf16[128,5120]{1,0:T(8,128)(2,1)}), bf16[16,5120]{1,0:T(8,128)(2,1)}) %reduce-scatter.3.cloned.1.call-update) | async-done | bytes 163856 | tf_op jit(solution)/shard_map/reduce_scatter | solution.py:66
  77.4 1.1 fusion.42
  78.5 1.7 %fusion.44 = bf16[16,5120]{1,0:T(8,128)(2,1)} fusion(f32[5120]{0:T(1024)S(1)} %convert_element_type.239, f32[16]{0:T(128)S(1)} %add_rsqrt_fusion, bf16[16,5120]{1,0:T(8,128)(2,1)} %reduce-scatter.3.cloned.1.call-done, bf16[16,5120]{1,0:T(8,128)(2,1)S(1)} %copy-done.1), kind=kLoop, calls=%fused_computation.71 | loop fusion | flops 655360 | bytes 512064 | tf_op jit(solution)/shard_map/convert_element_type | solution.py:10
  80.2 0.2 reduce-scatter.5.cloned.1.call-start
  80.5 21.6 %all-gather.5.cloned.1.call-done = bf16[128,5120]{1,0:T(8,128)(2,1)} async-done(((bf16[16,5120]{1,0:T(8,128)(2,1)}), bf16[128,5120]{1,0:T(8,128)(2,1)}) %all-gather.5.cloned.1.call-update) | async-done | bytes 1310736 | tf_op jit(solution)/shard_map/all_gather | solution.py:69
  102.1 11.1 %fusion.135 = f32[128,2176]{1,0:T(8,128)S(1)} fusion(bf16[128,5120]{1,0:T(8,128)(2,1)} %all-gather.5.cloned.1.call-done, bf16[5120,2176]{1,0:T(8,128)(2,1)} %param.17), kind=kOutput, calls=%fused_computation.229 | convolution fusion | flops 2852126720 | bytes 24707072 | tf_op jit(solution)/shard_map/dot_general | solution.py:70
  113.2 21.3 %convolution_convert_fusion = bf16[128,5120]{1,0:T(8,128)(2,1)} fusion(bf16[2176,5120]{1,0:T(8,128)(2,1)} %param.19, bf16[128,5120]{1,0:T(8,128)(2,1)S(1)} %copy-done.3, bf16[5120,2176]{1,0:T(8,128)(2,1)} %param.18, f32[128,2176]{1,0:T(8,128)S(1)} %fusion.135), kind=kOutput, calls=%fused_computation.2 | convolution fusion | flops 5706579968 | bytes 48300032 | tf_op jit(solution)/shard_map/dot_general | solution.py:73
  134.5 0.7 copy.52
  135.2 24.6 %reduce-scatter.5.cloned.1.call-done = bf16[16,5120]{1,0:T(8,128)(2,1)} async-done(((bf16[128,5120]{1,0:T(8,128)(2,1)}), bf16[16,5120]{1,0:T(8,128)(2,1)}) %reduce-scatter.5.cloned.1.call-update) | async-done | bytes 163856 | tf_op jit(solution)/shard_map/reduce_scatter | solution.py:74
  159.9 1.6 fusion.45
  (46 shorter events, 1.0 us)
Async XLA Ops:
  7.2 26.6 %all-gather.3.cloned.1.call-start = ((), (), s32[]{:S(2)}) async-start(), calls=%async_computation.2 | async-start | bytes 1474560 | tf_op jit(solution)/shard_map/all_gather | solution.py:56
  10.8 66.6 %reduce-scatter.3.cloned.1.call-start = ((), (), s32[]{:S(2)}) async-start(), calls=%async_computation.3 | async-start | bytes 1474560 | tf_op jit(solution)/shard_map/reduce_scatter | solution.py:66
  33.8 2.3 %copy-start = (bf16[128,5120]{1,0:T(8,128)(2,1)S(1)}, bf16[128,5120]{1,0:T(8,128)(2,1)}, u32[]{:S(2)}) copy-start(bf16[128,5120]{1,0:T(8,128)(2,1)} %all-gather.3.cloned.1.call-done) | copy-start | bytes 3932164
  36.0 11.3 %slice-start = ((s8[6553600]{0:T(1024)(128)(4,1)}), s8[4194304]{0:T(1024)(128)(4,1)S(1)}, s32[]{:S(2)}) async-start(s8[6553600]{0:T(1024)(128)(4,1)} %bitcast.242), calls=%async_computation.6 | async-start | bytes 8388608
  40.9 2.6 %copy-start.2 = (bf16[5120,1,128]{2,1,0:T(2,128)(2,1)S(1)}, bf16[5120,1,128]{2,1,0:T(2,128)(2,1)}, u32[]{:S(2)}) copy-start(bf16[5120,1,128]{2,1,0:T(2,128)(2,1)} %get-tuple-element.32) | copy-start | bytes 3932164
  41.0 6.4 %slice-start.1 = ((s8[6553600]{0:T(1024)(128)(4,1)}), s8[2359296]{0:T(1024)(128)(4,1)S(1)}, s32[]{:S(2)}) async-start(s8[6553600]{0:T(1024)(128)(4,1)} %bitcast.242), calls=%async_computation.7 | async-start | bytes 4718592
  44.1 5.6 %copy-start.6 = (bf16[128,128]{1,0:T(8,128)(2,1)}, bf16[128,128]{1,0:T(8,128)(2,1)S(1)}, u32[]{:S(2)}) copy-start(bf16[128,128]{1,0:T(8,128)(2,1)S(1)} %fusion.5) | copy-start | bytes 98308
  49.7 0.7 copy-start.5
  49.7 27.7 %copy-start.1 = (bf16[16,5120]{1,0:T(8,128)(2,1)S(1)}, bf16[16,5120]{1,0:T(8,128)(2,1)}, u32[]{:S(2)}) copy-start(bf16[16,5120]{1,0:T(8,128)(2,1)} %param.10) | copy-start | bytes 491524
  49.7 52.4 %all-gather.5.cloned.1.call-start = ((), (), s32[]{:S(2)}) async-start(), calls=%async_computation.4 | async-start | bytes 1474560 | tf_op jit(solution)/shard_map/all_gather | solution.py:69
  80.2 79.6 %reduce-scatter.5.cloned.1.call-start = ((), (), s32[]{:S(2)}) async-start(), calls=%async_computation.5 | async-start | bytes 1474560 | tf_op jit(solution)/shard_map/reduce_scatter | solution.py:74
  102.1 11.1 %copy-start.3 = (bf16[128,5120]{1,0:T(8,128)(2,1)S(1)}, bf16[128,5120]{1,0:T(8,128)(2,1)}, u32[]{:S(2)}) copy-start(bf16[128,5120]{1,0:T(8,128)(2,1)} %all-gather.5.cloned.1.call-done) | copy-start | bytes 3932164
  134.4 25.4 %copy-start.4 = (bf16[16,5120]{1,0:T(8,128)(2,1)S(1)}, bf16[16,5120]{1,0:T(8,128)(2,1)}, u32[]{:S(2)}) copy-start(bf16[16,5120]{1,0:T(8,128)(2,1)} %reduce-scatter.3.cloned.1.call-done) | copy-start | bytes 491524
Sparse Core Ops, SparseCore 0:
  10.9 22.8 all-gather.2
  49.8 27.4 reduce-scatter.2
  80.3 21.6 all-gather.4
  134.6 25.1 reduce-scatter.4
where the time goes:
time: 171 us; the launch traced here: 168 us
  waiting for transfers between devices  74.4 us (44%)
  matrix products  46.6 us (27%)
  local copies, waits for them, and re-layouts  22.5 us (13%)
  between operations  14.1 us (8%)
  other arithmetic  10.1 us (6%)
    reduce_scatter x1, waiting for transfers between devices, local_layer(): lax.psum_scatter(attn_part, 'tp', scatter_dimension=0, tiled=True)  27 us
    reduce_scatter x1, waiting for transfers between devices, local_layer(): mlp_sum = lax.psum_scatter(mlp_part, 'tp', scatter_dimension=0, tiled=True)  24.6 us
    all_gather x1, waiting for transfers between devices, local_layer(): gathered_mlp = lax.all_gather(normed_mlp, 'tp', axis=0, tiled=True)  21.6 us
    dot_general x1, matrix products, local_layer(): jnp.dot(mlp_act, w_down, preferred_element_type=jnp.float32)  21.3 us
    dynamic_slice x1, local copies, waits for them, and re-layouts, local_layer(): key_local = lax.dynamic_slice_in_dim(w_key, first_kv, kv_local, axis=1)  11.6 us
    dot_general x1, matrix products, local_layer(): jnp.dot(gathered_mlp, w_gate, preferred_element_type=jnp.float32)  11.1 us
    unnamed x20, local copies, waits for them, and re-layouts  10.9 us
    unnamed x1, matrix products  4.86 us
  transfers between devices with their start and end apart: 4, of which 4 were waited for; matrix products, arithmetic and copies ran while one was open for 13% of the time, Pallas kernels for 0%

commit v1 on v0

v1 whole, which is shorter than its diff:
```python
import functools

import jax
import jax.numpy as jnp
import numpy as np
from jax import lax
from jax.experimental import pallas as pl
from jax.experimental.pallas import tpu as pltpu
from jax.sharding import PartitionSpec as P

BF = jnp.bfloat16
F32 = jnp.float32
KC = 1024
RAW = 640
N_SLOTS = 9


def dot(a, b):
    return jnp.dot(a, b, preferred_element_type=F32)


def spans(width, step):
    return [(lo, min(step, width - lo)) for lo in range(0, width, step)]


def kernel(eps, hid_hbm, an_hbm, mn_hbm, cos_hbm, sin_hbm, wq_hbm, wk_hbm, wv_hbm, wo_hbm, wg_hbm, wu_hbm, wd_hbm,
           out_ref, kc_ref, vc_ref,
           hid, gain_a, gain_m, cos_t, sin_t, wq, wkv, raw, wo, slots, xg, acc, qs, ob, ub,
           pbuf, dbuf, leg_out, leg_in, ffd_out, ffs_out, fin_a, fin_b, mid, res,
           sem_small, sem_raw, sem_wq, sem_wo, sem_slot, sem_down,
           ag_send, ag_recv, rs_send, rs_recv):
    t = lax.axis_index("tp")
    c = t % 2
    x = t // 2
    n_chip = lax.axis_size("tp") // 2
    xf = (x + 1 + 2 * c) % n_chip
    xs = (x + 3 + 2 * c) % n_chip
    xo = (x + 2) % n_chip
    peer = 2 * x + 1 - c
    dev_f = 2 * xf + c
    dev_s = 2 * xs + c
    rows, width = hid.shape
    heads, depth, hd = wq.shape
    tokens = xg.shape[0]
    ff = ub.shape[1]
    n_chunk = width // KC

    def local(src, dst, sem):
        return pltpu.make_async_copy(src, dst, sem)

    small = [local(hid_hbm, hid, sem_small.at[0]), local(an_hbm, gain_a, sem_small.at[1]),
             local(mn_hbm, gain_m, sem_small.at[2]), local(cos_hbm, cos_t, sem_small.at[3]),
             local(sin_hbm, sin_t, sem_small.at[4])]
    for cp in small:
        cp.start()
    pair = x
    n_raw = depth // RAW

    def raw_copies(i):
        rng = pl.ds(i * RAW, RAW)
        return [local(wk_hbm.at[rng, pair], raw.at[i % 2, 0], sem_raw.at[i % 2, 0]),
                local(wv_hbm.at[rng, pair], raw.at[i % 2, 1], sem_raw.at[i % 2, 1])]

    for i in range(2):
        for cp in raw_copies(i):
            cp.start()
    wq_copy = local(wq_hbm, wq, sem_wq)
    wq_copy.start()
    wo_copy = local(wo_hbm, wo, sem_wo)
    wo_copy.start()
    def gu_copy(i):
        src = (wg_hbm, wu_hbm)[i % 2]
        return local(src.at[pl.ds((i // 2) * KC, KC)], slots.at[i % N_SLOTS], sem_slot.at[i])
    for i in range(N_SLOTS):
        gu_copy(i).start()

    barrier = pltpu.get_barrier_semaphore()
    for dev in (peer, dev_f, dev_s):
        pl.semaphore_signal(barrier, inc=1, device_id={"tp": dev}, device_id_type=pl.DeviceIdType.MESH)

    def remote(src, dst, ssem, rsem, dev):
        return pltpu.make_async_remote_copy(src_ref=src, dst_ref=dst, send_sem=ssem, recv_sem=rsem,
                                            device_id={"tp": dev}, device_id_type=pl.DeviceIdType.MESH)

    def block(b, k):
        return xg.at[pl.ds(pl.multiple_of(b * rows, rows), rows), pl.ds(k * KC, KC)]

    def ag_copy(g, k, j):
        b, dev = [(t, dev_f), (t, dev_s), (t, peer), (dev_s, dev_f), (dev_s, peer), (dev_f, peer),
                  (2 * xo + c, peer)][j]
        return remote(block(b, k), block(b, k), ag_send.at[g, k, j], ag_recv.at[g, k, j], dev)

    def ag_arrival(g, k, j):
        b = [dev_s, dev_f, peer, 2 * xo + c, 2 * xs + 1 - c, 2 * xf + 1 - c, 2 * xo + 1 - c]
        b[4], b[5] = b[5], b[4]
        return remote(block(b[j], k), block(b[j], k), ag_send.at[g, k, j], ag_recv.at[g, k, j], peer)

    def ag_own(g, k):
        for j in range(3):
            ag_copy(g, k, j).start()

    def ag_relay(g, k):
        ag_arrival(g, k, 0).wait_recv()
        ag_copy(g, k, 3).start()
        ag_copy(g, k, 4).start()
        ag_arrival(g, k, 1).wait_recv()
        ag_copy(g, k, 5).start()

    def ag_relay2(g, k):
        ag_arrival(g, k, 3).wait_recv()
        ag_copy(g, k, 6).start()

    def ag_finish(g, k):
        for j in (2, 4, 5, 6):
            ag_arrival(g, k, j).wait_recv()

    def gather(g, compute, fill=lambda n: None):
        ag_own(g, 0)
        ag_own(g, 1)
        ag_own(g, 2)
        fill(3)
        ag_relay(g, 0)
        ag_own(g, 3)
        fill(1)
        ag_relay(g, 1)
        ag_own(g, 4)
        fill(1)
        ag_relay(g, 2)
        fill(1)
        ag_relay2(g, 0)
        fill(2)
        ag_finish(g, 0)
        compute(0)
        ag_relay(g, 3)
        ag_relay2(g, 1)
        ag_relay(g, 4)
        ag_relay2(g, 2)
        ag_finish(g, 1)
        compute(1)
        ag_relay2(g, 3)
        ag_relay2(g, 4)
        for k in range(2, n_chunk):
            ag_finish(g, k)
            compute(k)
        for k in range(n_chunk):
            for j in range(7):
                ag_copy(g, k, j).wait_send()

    cuts = [(lo + a, s) for lo, w in spans(width, ff) for a, s in spans(w, 9 * 128)]

    def rs_copy(g, i, j):
        lo, size = cuts[i]
        col = pl.ds(lo, size)
        src, dst, dev = [(pbuf.at[:, 1 - c, :, col], dbuf.at[:, :, col], peer),
                         (leg_out.at[:, col], leg_in.at[:, col], dev_f),
                         (ffs_out.at[:, col], fin_b.at[:, col], dev_s),
                         (ffd_out.at[:, col], fin_a.at[:, col], dev_f)][j]
        return remote(src, dst, rs_send.at[g, i, j], rs_recv.at[g, i, j], dev)

    def reduce_scatter(g, product, lag, finish):
        n = len(cuts)

        def make(i):
            lo, size = cuts[i]
            for a, s in spans(size, 256):
                pbuf[:, :, :, lo + a:lo + a + s] = product(lo + a, s).astype(BF).reshape(tokens // (2 * rows), 2, rows, s)
            rs_copy(g, i, 0).start()

        def chip_sum(d, lo, size):
            return pbuf[d, c, :, lo:lo + size].astype(F32) + dbuf[d, :, lo:lo + size].astype(F32)

        def combine(i):
            lo, size = cuts[i]
            rs_copy(g, i, 0).wait_recv()
            leg_out[:, lo:lo + size] = chip_sum(xo, lo, size).astype(BF)
            ffs_out[:, lo:lo + size] = chip_sum(xs, lo, size).astype(BF)
            rs_copy(g, i, 1).start()
            rs_copy(g, i, 2).start()

        def relay(i):
            lo, size = cuts[i]
            rs_copy(g, i, 1).wait_recv()
            ffd_out[:, lo:lo + size] = (chip_sum(xf, lo, size) + leg_in[:, lo:lo + size].astype(F32)).astype(BF)
            rs_copy(g, i, 3).start()

        def last(i):
            lo, size = cuts[i]
            rs_copy(g, i, 2).wait_recv()
            rs_copy(g, i, 3).wait_recv()
            total = (chip_sum(x, lo, size) + fin_a[:, lo:lo + size].astype(F32)
                     + fin_b[:, lo:lo + size].astype(F32))
            finish(lo, size, total)

        for i in range(n + lag):
            if i < n:
                make(i)
            if i >= lag:
                combine(i - lag)
        for i in range(n):
            relay(i)
        for i in range(n):
            last(i)
        for i in range(n):
            for j in range(4):
                rs_copy(g, i, j).wait_send()

    def normalize(src, gain, sum_sq):
        scale = lax.rsqrt(sum_sq * (1.0 / width) + eps)
        for lo, size in spans(width, KC):
            xg[pl.ds(pl.multiple_of(t * rows, rows), rows), lo:lo + size] = (
                src[:, lo:lo + size].astype(F32) * scale * gain[:, lo:lo + size].astype(F32)).astype(BF)

    for cp in small:
        cp.wait()
    sum_sq = jnp.zeros((rows, 1), F32)
    for lo, size in spans(width, KC):
        part = hid[:, lo:lo + size].astype(F32)
        sum_sq = sum_sq + jnp.sum(part * part, axis=-1, keepdims=True)
    normalize(hid, gain_a, sum_sq)
    pl.semaphore_wait(barrier, 3)

    row = lax.broadcasted_iota(jnp.int32, (128, 256), 0)
    col = lax.broadcasted_iota(jnp.int32, (128, 256), 1)
    pick = jnp.where(col == 2 * row + c, 1.0, 0.0).astype(BF)
    todo = list(range(n_raw))

    def select_heads(count):
        for _ in range(count):
            i = todo.pop(0)
            for cp in raw_copies(i):
                cp.wait()
            for a in range(RAW // 128):
                both = jnp.concatenate([raw[i % 2, j, 128 * a:128 * a + 128].reshape(256, hd) for j in range(2)], axis=1)
                wkv[i * RAW + 128 * a:i * RAW + 128 * a + 128, :] = dot(pick, both).astype(BF)
            if i + 2 < n_raw:
                for cp in raw_copies(i + 2):
                    cp.start()

    nq = heads * hd

    def qkv(k):
        if k == 0:
            select_heads(len(todo))
            wq_copy.wait()
        r = slice(k * KC, k * KC + KC)
        a = xg[:, r]
        for h in range(0, heads, 2):
            if h + 1 < heads:
                w = jnp.concatenate([wq[h, r, :], wq[h + 1, r, :]], axis=1)
            else:
                w = wq[h, r, :]
            part = dot(a, w)
            lo, hi = h * hd, h * hd + w.shape[1]
            acc[:, lo:hi] = part if k == 0 else acc[:, lo:hi] + part
        part = dot(a, wkv[r, :])
        acc[:, nq:nq + 2 * hd] = part if k == 0 else acc[:, nq:nq + 2 * hd] + part

    gather(0, qkv, select_heads)

    def rope(v):
        return v * cos_t[...] + jnp.concatenate([v[:, hd // 2:], v[:, :hd // 2]], axis=1) * sin_t[...]

    for h in range(heads):
        qs[h * tokens:h * tokens + tokens, :] = rope(acc[:, h * hd:h * hd + hd]).astype(BF)
    k_rot = rope(acc[:, nq:nq + hd]).astype(BF)
    v_loc = acc[:, nq + hd:nq + 2 * hd].astype(BF)
    kc_ref[...] = k_rot
    vc_ref[...] = v_loc
    seen = (lax.broadcasted_iota(jnp.int32, (tokens, tokens), 1)
            <= lax.broadcasted_iota(jnp.int32, (tokens, tokens), 0))
    for h in range(heads):
        s = lax.dot_general(qs[h * tokens:h * tokens + tokens, :], k_rot, (((1,), (1,)), ((), ())),
                            preferred_element_type=F32) * (hd ** -0.5)
        s = jnp.where(seen, s, -1e30)
        e = jnp.exp(s - jnp.max(s, axis=-1, keepdims=True))
        p = (e / jnp.sum(e, axis=-1, keepdims=True)).astype(BF)
        ob[:, h * hd:h * hd + hd] = dot(p, v_loc).astype(BF)

    wo_copy.wait()
    sq = [jnp.zeros((rows, 1), F32)]

    def mid_finish(lo, size, total):
        m = (hid[:, lo:lo + size].astype(F32) + total).astype(BF)
        mid[:, lo:lo + size] = m
        m = m.astype(F32)
        sq[0] = sq[0] + jnp.sum(m * m, axis=-1, keepdims=True)

    reduce_scatter(0, lambda lo, size: dot(ob[...], wo[:, lo:lo + size]), 3, mid_finish)

    down0 = local(wd_hbm.at[pl.ds(0, nq)], wo, sem_down.at[0])
    down0.start()
    tail = [(nq, KC), (nq + KC, ff - nq - KC)]
    pieces = [(r, n, lo, s) for lo, s in spans(width, ff) for r, n in tail]
    free = [s % N_SLOTS for s in range(2 * n_chunk)][:2 * (n_chunk - 1)]
    order = [i for i in range(2 * (n_chunk - 1))][2 * n_chunk - N_SLOTS:]
    place = [(p, order[i] % N_SLOTS, i) for i, p in enumerate(pieces)]

    def piece_copy(i):
        (r, n, lo, s), slot, j = place[i]
        return local(wd_hbm.at[pl.ds(r, n), pl.ds(lo, s)], slots.at[slot, pl.ds(0, n), pl.ds(0, s)], sem_down.at[1 + j])

    normalize(mid, gain_m, sq[0])

    def gate_up(k):
        a = xg[:, k * KC:k * KC + KC]
        for half in range(2):
            i = 2 * k + half
            gu_copy(i).wait()
            for lo, s in spans(ff, 256):
                part = dot(a, slots[i % N_SLOTS, :, lo:lo + s])
                lo2 = half * ff + lo
                acc[:, lo2:lo2 + s] = part if k == 0 else acc[:, lo2:lo2 + s] + part
            if i + N_SLOTS < 2 * n_chunk:
                gu_copy(i + N_SLOTS).start()
            for j in range(len(place)):
                if order[j] == i:
                    piece_copy(j).start()

    gather(1, gate_up)

    for lo, s in spans(ff, 256):
        g = acc[:, lo:lo + s]
        ub[:, lo:lo + s] = (g * (1.0 / (1.0 + jnp.exp(-g))) * acc[:, ff + lo:ff + lo + s]).astype(BF)
    down0.wait()
    got = set()

    def down(lo, size):
        total = dot(ub[:, :nq], wo[:, lo:lo + size])
        for i, ((r, n, plo, ps), slot, j) in enumerate(place):
            if plo <= lo < plo + ps:
                if i not in got:
                    got.add(i)
                    piece_copy(i).wait()
                total = total + dot(ub[:, r:r + n], slots[slot, :n, lo - plo:lo - plo + size])
        return total

    def out_finish(lo, size, total):
        out_ref[:, lo:lo + size] = (mid[:, lo:lo + size].astype(F32) + total).astype(BF)

    reduce_scatter(1, down, 1, out_finish)


def solution(mesh):
    tp_size = mesh.shape["tp"]

    def local_layer(hidden_in, attn_norm, mlp_norm, w_query, w_key, w_value, w_out, w_gate, w_up, w_down):
        rows, width = hidden_in.shape
        tokens = rows * tp_size
        heads, hd = w_query.shape[1:]
        kv_heads = w_key.shape[1]
        ff = w_gate.shape[1]
        half = hd // 2
        freq = (1.0 / (np.float32(500000.0) ** (np.arange(half, dtype=np.float32) * np.float32(2.0 / hd)))).astype(np.float32)
        angle = (np.arange(tokens, dtype=np.float32)[:, None] * freq[None, :]).astype(np.float32)
        cos = np.cos(angle.astype(np.float64)).astype(np.float32)
        sin = np.sin(angle.astype(np.float64)).astype(np.float32)
        cos = jnp.asarray(np.concatenate([cos, cos], axis=1))
        sin = jnp.asarray(np.concatenate([-sin, sin], axis=1))
        n_cut = len([1 for _, w in spans(width, ff) for _ in spans(w, 9 * 128)])
        n_chunk = width // KC
        any_spec = pl.BlockSpec(memory_space=pl.ANY)
        vmem = pl.BlockSpec(memory_space=pltpu.VMEM)
        row_buf = pltpu.VMEM((rows, width), BF)
        dma = pltpu.SemaphoreType.DMA
        out, k_cache, v_cache = pl.pallas_call(
            functools.partial(kernel, 1e-5),
            out_shape=(jax.ShapeDtypeStruct((rows, width), BF), jax.ShapeDtypeStruct((tokens, hd), BF),
                       jax.ShapeDtypeStruct((tokens, hd), BF)),
            in_specs=[any_spec] * 12,
            out_specs=(vmem, vmem, vmem),
            scratch_shapes=[
                row_buf, pltpu.VMEM((1, width), BF), pltpu.VMEM((1, width), BF),
                pltpu.VMEM((tokens, hd), F32), pltpu.VMEM((tokens, hd), F32),
                pltpu.VMEM((heads, width, hd), BF), pltpu.VMEM((width, 2 * hd), BF),
                pltpu.VMEM((2, 2, RAW, 2, hd), BF), pltpu.VMEM((heads * hd, width), BF),
                pltpu.VMEM((N_SLOTS, KC, ff), BF), pltpu.VMEM((tokens, width), BF),
                pltpu.VMEM((tokens, 2 * ff), F32), pltpu.VMEM((heads * tokens, hd), BF),
                pltpu.VMEM((tokens, heads * hd), BF), pltpu.VMEM((tokens, ff), BF),
                pltpu.VMEM((tp_size // 2, 2, rows, width), BF), pltpu.VMEM((tp_size // 2, rows, width), BF),
                row_buf, row_buf, row_buf, row_buf, row_buf, row_buf, row_buf, pltpu.VMEM((8, 128), F32),
                dma((5,)), dma((2, 2)), dma(()), dma(()), dma((2 * n_chunk,)), dma((8,)),
                dma((2, n_chunk, 7)), dma((2, n_chunk, 7)), dma((2, n_cut, 4)), dma((2, n_cut, 4)),
            ],
            compiler_params=pltpu.CompilerParams(collective_id=0, has_side_effects=True, vmem_limit_bytes=67_043_328),
        )(hidden_in, attn_norm.reshape(1, width), mlp_norm.reshape(1, width), cos, sin,
          jnp.transpose(w_query, (1, 0, 2)), w_key.reshape(width, kv_heads // 2, 2, hd),
          w_value.reshape(width, kv_heads // 2, 2, hd), w_out.reshape(heads * hd, width), w_gate, w_up, w_down)
        return out, k_cache.reshape(tokens, 1, hd), v_cache.reshape(tokens, 1, hd)

    row_spec = P(("dp", "tp"), None)
    cache_spec = P("dp", "tp", None)
    return jax.shard_map(local_layer, mesh=mesh, in_specs=(row_spec, P(), P(), P(None, "tp", None), P(), P(), P("tp", None, None), P(None, "tp"), P(None, "tp"), P("tp", None)), out_specs=(row_spec, cache_spec, cache_spec), check_vma=False)
```

time: 171 us -> 81.8 us (0.48)
  waiting for transfers between devices: 74.4 us -> 0 us
  Pallas kernels: 0 us -> 72.7 us
  matrix products: 46.6 us -> 0 us
  local copies, waits for them, and re-layouts: 22.5 us -> 6.98 us
  between operations: 14.1 us -> 0.64 us
  other arithmetic: 10.1 us -> 0 us
    pallas_call x0 -> x1, Pallas kernels: none -> 72.7 us  [local_layer(): pl.pallas_call(functools.partial(kernel, 1e-05), out_shape=(jax.ShapeDtyp...]
    reduce_scatter x2 -> x0, waiting for transfers between devices: 51.6 us -> none  [the longest x1 27 us: local_layer(): lax.psum_scatter(attn_part, 'tp', scatter_dimension=0, tiled=True)]
    dot_general x21 -> x0, matrix products: 41.7 us -> none  [the longest x1 21.3 us: local_layer(): jnp.dot(mlp_act, w_down, preferred_element_type=jnp.float32)]
    all_gather x2 -> x0, waiting for transfers between devices: 22.5 us -> none  [the longest x1 21.6 us: local_layer(): gathered_mlp = lax.all_gather(normed_mlp, 'tp', axis=0, tiled=True)]
    dynamic_slice x1 -> x0, local copies, waits for them, and re-layouts: 11.6 us -> none  [local_layer(): key_local = lax.dynamic_slice_in_dim(w_key, first_kv, kv_local, axis=1)]
    unnamed x20 -> x3, local copies, waits for them, and re-layouts: 10.9 us -> 4.34 us
    convert_element_type x6 -> x0, other arithmetic: 5.74 us -> none  [the longest x2 3.38 us: rms_norm(): (rows_f * lax.rsqrt(mean_sq + 1e-05) * gain_vec.astype(jnp.float32)).asty...]
    unnamed x1 -> x0, matrix products: 4.86 us -> none
  transfers between devices with their start and end apart: 4 -> 0, of which waited for: 4 -> 0; matrix products, arithmetic and copies ran while one was open for 13% -> 0% of each run, Pallas kernels for 0% -> 0%
where the time goes in v1:
time: 81.8 us; the launch traced here: 80.4 us
  Pallas kernels  72.7 us (89%)
  local copies, waits for them, and re-layouts  6.98 us (9%)
    pallas_call x1, Pallas kernels, local_layer(): pl.pallas_call(functools.partial(kernel, 1e-05), out_shape=(jax.ShapeDtyp...  72.7 us
    unnamed x3, local copies, waits for them, and re-layouts  4.34 us

profile of v1, /device:TPU:113, one launch (start us, length us, event | category | flops | bytes accessed | tf_op | source)
XLA Modules:
  0.0 80.4 jit_solution(8366287369819311451)
XLA Ops:
  0.6 1.3 %reshape.27.an_hbm = bf16[1,5120]{1,0:T(2,128)(2,1)} reshape(bf16[5120]{0:T(1024)(128)(2,1)} %param.13) | data formatting | bytes 20480 | tf_op jit(solution)/shard_map/reshape | solution.py:385
  2.0 1.3 %reshape.28.mn_hbm = bf16[1,5120]{1,0:T(2,128)(2,1)} reshape(bf16[5120]{0:T(1024)(128)(2,1)} %param.14) | data formatting | bytes 20480 | tf_op jit(solution)/shard_map/reshape | solution.py:385
  3.3 72.7 %shard_map.139 = (bf16[16,5120]{1,0:T(8,128)(2,1)}, bf16[128,128]{1,0:T(8,128)(2,1)}, bf16[128,128]{1,0:T(8,128)(2,1)}) custom-call(bf16[16,5120]{1,0:T(8,128)(2,1)} %hid_hbm.1, bf16[1,5120]{1,0:T(2,128)(2,1)} %reshape.27.an_hbm, bf16[1,5120]{1,0:T(2,128)(2,1)} %reshape.28.mn_hbm, f32[128,128]{1,0:T(8,128)} %constant.4.clone.cos_hbm, ...), custom_call_target="tpu_custom_call" | custom-call | tf_op jit(solution)/shard_map/pallas_call | solution.py:365
  76.0 1.6 %copy.18 = bf16[16,5120]{1,0:T(8,128)(2,1)} copy(bf16[16,5120]{1,0:T(8,128)(2,1)} %get-tuple-element.12) | data formatting | bytes 327680
  77.6 1.4 %copy.19 = bf16[128,1,128]{2,0,1:T(8,128)(2,1)} copy(bf16[128,1,128]{2,0,1:T(8,128)(2,1)} %bitcast.11) | data formatting | bytes 65536
  79.0 1.4 %copy.20 = bf16[128,1,128]{2,0,1:T(8,128)(2,1)} copy(bf16[128,1,128]{2,0,1:T(8,128)(2,1)} %bitcast.10) | data formatting | bytes 65536

commit v2 on v1

v2 whole, which is shorter than its diff:
```python
import functools

import jax
import jax.numpy as jnp
import numpy as np
from jax import lax
from jax.experimental import pallas as pl
from jax.experimental.pallas import tpu as pltpu
from jax.sharding import PartitionSpec as P

BF = jnp.bfloat16
F32 = jnp.float32
KC = 1024
RAW = 640
N_SLOTS = 9


def dot(a, b):
    return jnp.dot(a, b, preferred_element_type=F32)


def spans(width, step):
    return [(lo, min(step, width - lo)) for lo in range(0, width, step)]


def kernel(eps, hid_hbm, an_hbm, mn_hbm, cos_hbm, sin_hbm, wq_hbm, wk_hbm, wv_hbm, wo_hbm, wg_hbm, wu_hbm, wd_hbm,
           out_ref, kc_ref, vc_ref,
           hid, gain_a, gain_m, cos_t, sin_t, wq, wkv, wo, slots, xg, qacc, qs, ob,
           dbuf, leg_in, fin_a, fin_b, mid,
           sem_small, sem_raw, sem_wq, sem_wo, sem_slot, sem_down,
           ag_send, ag_recv, rs_send, rs_recv):
    t = lax.axis_index("tp")
    c = t % 2
    x = t // 2
    n_chip = lax.axis_size("tp") // 2
    xf = (x + 1 + 2 * c) % n_chip
    xs = (x + 3 + 2 * c) % n_chip
    xo = (x + 2) % n_chip
    peer = 2 * x + 1 - c
    dev_f = 2 * xf + c
    dev_s = 2 * xs + c
    rows, width = hid.shape
    heads, depth, hd = wq.shape
    tokens = xg.shape[0]
    ff = slots.shape[2]
    n_chunk = width // KC

    def local(src, dst, sem):
        return pltpu.make_async_copy(src, dst, sem)

    small = [local(hid_hbm, hid, sem_small.at[0]), local(an_hbm, gain_a, sem_small.at[1]),
             local(mn_hbm, gain_m, sem_small.at[2]), local(cos_hbm, cos_t, sem_small.at[3]),
             local(sin_hbm, sin_t, sem_small.at[4])]
    for cp in small:
        cp.start()
    pair = x
    n_raw = depth // RAW

    wq_copy = local(wq_hbm, wq, sem_wq)
    wo_copy = local(wo_hbm, wo, sem_wo)

    def gu_copy(i):
        src = (wg_hbm, wu_hbm)[i % 2]
        return local(src.at[pl.ds((i // 2) * KC, KC)], slots.at[i % N_SLOTS], sem_slot.at[i])

    def remote(src, dst, ssem, rsem, dev):
        return pltpu.make_async_remote_copy(src_ref=src, dst_ref=dst, send_sem=ssem, recv_sem=rsem,
                                            device_id={"tp": dev}, device_id_type=pl.DeviceIdType.MESH)

    def block(b, k):
        return xg.at[pl.ds(pl.multiple_of(b * rows, rows), rows), pl.ds(k * KC, KC)]

    def ag_copy(g, k, j):
        b, dev = [(t, dev_f), (t, dev_s), (t, peer), (dev_s, dev_f), (dev_s, peer), (dev_f, peer),
                  (2 * xo + c, peer)][j]
        return remote(block(b, k), block(b, k), ag_send.at[g, k, j], ag_recv.at[g, k, j], dev)

    def ag_arrival(g, k, j):
        b = [dev_s, dev_f, peer, 2 * xo + c, 2 * xs + 1 - c, 2 * xf + 1 - c, 2 * xo + 1 - c]
        b[4], b[5] = b[5], b[4]
        return remote(block(b[j], k), block(b[j], k), ag_send.at[g, k, j], ag_recv.at[g, k, j], peer)

    def ag_own(g, k):
        for j in range(3):
            ag_copy(g, k, j).start()

    def ag_relay(g, k):
        ag_arrival(g, k, 0).wait_recv()
        ag_copy(g, k, 3).start()
        ag_copy(g, k, 4).start()
        ag_arrival(g, k, 1).wait_recv()
        ag_copy(g, k, 5).start()

    def ag_relay2(g, k):
        ag_arrival(g, k, 3).wait_recv()
        ag_copy(g, k, 6).start()

    def ag_finish(g, k):
        for j in (2, 4, 5, 6):
            ag_arrival(g, k, j).wait_recv()

    def gather(g, compute, fill=lambda n: None):
        ag_own(g, 0)
        ag_own(g, 1)
        ag_own(g, 2)
        fill(3)
        ag_relay(g, 0)
        ag_own(g, 3)
        fill(1)
        ag_relay(g, 1)
        ag_own(g, 4)
        fill(1)
        ag_relay(g, 2)
        fill(1)
        ag_relay2(g, 0)
        fill(2)
        ag_finish(g, 0)
        compute(0)
        ag_relay(g, 3)
        ag_relay2(g, 1)
        ag_relay(g, 4)
        ag_relay2(g, 2)
        ag_finish(g, 1)
        compute(1)
        ag_relay2(g, 3)
        ag_relay2(g, 4)
        for k in range(2, n_chunk):
            ag_finish(g, k)
            compute(k)
        for k in range(n_chunk):
            for j in range(7):
                ag_copy(g, k, j).wait_send()

    cuts = [(lo + a, s) for lo, w in spans(width, ff) for a, s in spans(w, 9 * 128)]

    def normalize(src, gain, sum_sq):
        scale = lax.rsqrt(sum_sq * (1.0 / width) + eps)
        rows_f = gain[...].astype(F32)
        for i in range(width // 128):
            cols = slice(i * 128, i * 128 + 128)
            xg[pl.ds(pl.multiple_of(t * rows, rows), rows), cols] = (
                src[:, cols].astype(F32) * scale * rows_f[i:i + 1, :]).astype(BF)

    nq = heads * hd

    def first_part(raw):
        def raw_copies(i):
            rng = pl.ds(i * RAW, RAW)
            return [local(wk_hbm.at[rng, pair], raw.at[0, rng], sem_raw.at[i, 0]),
                    local(wv_hbm.at[rng, pair], raw.at[1, rng], sem_raw.at[i, 1])]

        for i in range(n_raw):
            for cp in raw_copies(i):
                cp.start()
        wq_copy.start()
        wo_copy.start()
        for i in range(N_SLOTS):
            gu_copy(i).start()

        barrier = pltpu.get_barrier_semaphore()
        for dev in (peer, dev_f, dev_s):
            pl.semaphore_signal(barrier, inc=1, device_id={"tp": dev}, device_id_type=pl.DeviceIdType.MESH)

        for cp in small:
            cp.wait()
        sum_sq = jnp.zeros((rows, 1), F32)
        for lo, size in spans(width, KC):
            part = hid[:, lo:lo + size].astype(F32)
            sum_sq = sum_sq + jnp.sum(part * part, axis=-1, keepdims=True)
        normalize(hid, gain_a, sum_sq)
        pl.semaphore_wait(barrier, 3)

        row = lax.broadcasted_iota(jnp.int32, (128, 256), 0)
        col = lax.broadcasted_iota(jnp.int32, (128, 256), 1)
        pick = jnp.where(col == 2 * row + c, 1.0, 0.0).astype(BF)
        todo = list(range(n_raw))

        def select_heads(count):
            for _ in range(count):
                i = todo.pop(0)
                for cp in raw_copies(i):
                    cp.wait()
                for a in range(RAW // 128):
                    both = jnp.concatenate([raw[j, i * RAW + 128 * a:i * RAW + 128 * a + 128].reshape(256, hd) for j in range(2)], axis=1)
                    wkv[i * RAW + 128 * a:i * RAW + 128 * a + 128, :] = dot(pick, both).astype(BF)


        def qkv(k):
            if k == 0:
                select_heads(len(todo))
                wq_copy.wait()
            r = slice(k * KC, k * KC + KC)
            a = xg[:, r]
            for h in range(0, heads, 2):
                if h + 1 < heads:
                    w = jnp.concatenate([wq[h, r, :], wq[h + 1, r, :]], axis=1)
                else:
                    w = wq[h, r, :]
                part = dot(a, w)
                lo, hi = h * hd, h * hd + w.shape[1]
                qacc[:, lo:hi] = part if k == 0 else qacc[:, lo:hi] + part
            part = dot(a, wkv[r, :])
            qacc[:, nq:nq + 2 * hd] = part if k == 0 else qacc[:, nq:nq + 2 * hd] + part

        gather(0, qkv, select_heads)


    pl.run_scoped(first_part, pltpu.VMEM((2, depth, 2, hd), BF))

    def rope(v):
        return v * cos_t[...] + jnp.concatenate([v[:, hd // 2:], v[:, :hd // 2]], axis=1) * sin_t[...]

    for h in range(heads):
        qs[h * tokens:h * tokens + tokens, :] = rope(qacc[:, h * hd:h * hd + hd]).astype(BF)
    k_rot = rope(qacc[:, nq:nq + hd]).astype(BF)
    v_loc = qacc[:, nq + hd:nq + 2 * hd].astype(BF)
    kc_ref[...] = k_rot
    vc_ref[...] = v_loc
    seen = (lax.broadcasted_iota(jnp.int32, (tokens, tokens), 1)
            <= lax.broadcasted_iota(jnp.int32, (tokens, tokens), 0))
    for h in range(heads):
        s = lax.dot_general(qs[h * tokens:h * tokens + tokens, :], k_rot, (((1,), (1,)), ((), ())),
                            preferred_element_type=F32) * (hd ** -0.5)
        s = jnp.where(seen, s, -1e30)
        e = jnp.exp(s - jnp.max(s, axis=-1, keepdims=True))
        p = (e / jnp.sum(e, axis=-1, keepdims=True)).astype(BF)
        ob[:, h * hd:h * hd + hd] = dot(p, v_loc).astype(BF)

    def second_part(acc, ub, pbuf, leg_out, ffd_out, ffs_out):
        def rs_copy(g, i, j):
            lo, size = cuts[i]
            col = pl.ds(lo, size)
            src, dst, dev = [(pbuf.at[:, 1 - c, :, col], dbuf.at[:, :, col], peer),
                             (leg_out.at[:, col], leg_in.at[:, col], dev_f),
                             (ffs_out.at[:, col], fin_b.at[:, col], dev_s),
                             (ffd_out.at[:, col], fin_a.at[:, col], dev_f)][j]
            return remote(src, dst, rs_send.at[g, i, j], rs_recv.at[g, i, j], dev)

        def reduce_scatter(g, product, lag, finish):
            n = len(cuts)

            def make(i):
                lo, size = cuts[i]
                for a, s in spans(size, 256):
                    pbuf[:, :, :, lo + a:lo + a + s] = product(lo + a, s).astype(BF).reshape(tokens // (2 * rows), 2, rows, s)
                rs_copy(g, i, 0).start()

            def chip_sum(d, lo, size):
                return pbuf[d, c, :, lo:lo + size].astype(F32) + dbuf[d, :, lo:lo + size].astype(F32)

            def combine(i):
                lo, size = cuts[i]
                rs_copy(g, i, 0).wait_recv()
                leg_out[:, lo:lo + size] = chip_sum(xo, lo, size).astype(BF)
                ffs_out[:, lo:lo + size] = chip_sum(xs, lo, size).astype(BF)
                rs_copy(g, i, 1).start()
                rs_copy(g, i, 2).start()

            def relay(i):
                lo, size = cuts[i]
                rs_copy(g, i, 1).wait_recv()
                ffd_out[:, lo:lo + size] = (chip_sum(xf, lo, size) + leg_in[:, lo:lo + size].astype(F32)).astype(BF)
                rs_copy(g, i, 3).start()

            def last(i):
                lo, size = cuts[i]
                rs_copy(g, i, 2).wait_recv()
                rs_copy(g, i, 3).wait_recv()
                total = (chip_sum(x, lo, size) + fin_a[:, lo:lo + size].astype(F32)
                         + fin_b[:, lo:lo + size].astype(F32))
                finish(lo, size, total)

            for i in range(n + lag):
                if i < n:
                    make(i)
                if i >= lag:
                    combine(i - lag)
            for i in range(n):
                relay(i)
            for i in range(n):
                last(i)
            for i in range(n):
                for j in range(4):
                    rs_copy(g, i, j).wait_send()

        wo_copy.wait()
        sq = [jnp.zeros((rows, 1), F32)]

        def mid_finish(lo, size, total):
            m = (hid[:, lo:lo + size].astype(F32) + total).astype(BF)
            mid[:, lo:lo + size] = m
            m = m.astype(F32)
            sq[0] = sq[0] + jnp.sum(m * m, axis=-1, keepdims=True)

        reduce_scatter(0, lambda lo, size: dot(ob[...], wo[:, lo:lo + size]), 3, mid_finish)

        down0 = local(wd_hbm.at[pl.ds(0, nq)], wo, sem_down.at[0])
        down0.start()
        tail = [(nq, KC), (nq + KC, ff - nq - KC)]
        pieces = [(r, n, lo, s) for lo, s in spans(width, ff) for r, n in tail]
        free = [s % N_SLOTS for s in range(2 * n_chunk)][:2 * (n_chunk - 1)]
        order = [i for i in range(2 * (n_chunk - 1))][2 * n_chunk - N_SLOTS:]
        place = [(p, order[i] % N_SLOTS, i) for i, p in enumerate(pieces)]

        def piece_copy(i):
            (r, n, lo, s), slot, j = place[i]
            return local(wd_hbm.at[pl.ds(r, n), pl.ds(lo, s)], slots.at[slot, pl.ds(0, n), pl.ds(0, s)], sem_down.at[1 + j])

        normalize(mid, gain_m, sq[0])

        def gate_up(k):
            a = xg[:, k * KC:k * KC + KC]
            for half in range(2):
                i = 2 * k + half
                gu_copy(i).wait()
                for lo, s in spans(ff, 256):
                    part = dot(a, slots[i % N_SLOTS, :, lo:lo + s])
                    lo2 = half * ff + lo
                    acc[:, lo2:lo2 + s] = part if k == 0 else acc[:, lo2:lo2 + s] + part
                if i + N_SLOTS < 2 * n_chunk:
                    gu_copy(i + N_SLOTS).start()
                for j in range(len(place)):
                    if order[j] == i:
                        piece_copy(j).start()

        gather(1, gate_up)

        for lo, s in spans(ff, 256):
            g = acc[:, lo:lo + s]
            ub[:, lo:lo + s] = (g * (1.0 / (1.0 + jnp.exp(-g))) * acc[:, ff + lo:ff + lo + s]).astype(BF)
        down0.wait()
        got = set()

        def down(lo, size):
            total = dot(ub[:, :nq], wo[:, lo:lo + size])
            for i, ((r, n, plo, ps), slot, j) in enumerate(place):
                if plo <= lo < plo + ps:
                    if i not in got:
                        got.add(i)
                        piece_copy(i).wait()
                    total = total + dot(ub[:, r:r + n], slots[slot, :n, lo - plo:lo - plo + size])
            return total

        def out_finish(lo, size, total):
            out_ref[:, lo:lo + size] = (mid[:, lo:lo + size].astype(F32) + total).astype(BF)

        reduce_scatter(1, down, 1, out_finish)

    row_buf = pltpu.VMEM((rows, width), BF)
    pl.run_scoped(second_part, pltpu.VMEM((tokens, 2 * ff), F32), pltpu.VMEM((tokens, ff), BF),
                  pltpu.VMEM((n_chip, 2, rows, width), BF), row_buf, row_buf, row_buf)


def hand_over(*refs):
    n = len(refs) // 3
    src, dst, buf, sem = refs[:n], refs[n:2 * n], refs[2 * n:3 * n], refs[3 * n]
    ins = [pltpu.make_async_copy(src[i], buf[i], sem.at[0, i]) for i in range(n)]
    outs = [pltpu.make_async_copy(buf[i], dst[i], sem.at[1, i]) for i in range(n)]
    for cp in ins:
        cp.start()
    for i in range(n):
        ins[i].wait()
        outs[i].start()
    for cp in outs:
        cp.wait()


def solution(mesh):
    tp_size = mesh.shape["tp"]

    def local_layer(hidden_in, attn_norm, mlp_norm, w_query, w_key, w_value, w_out, w_gate, w_up, w_down):
        rows, width = hidden_in.shape
        tokens = rows * tp_size
        heads, hd = w_query.shape[1:]
        kv_heads = w_key.shape[1]
        ff = w_gate.shape[1]
        half = hd // 2
        freq = (1.0 / (np.float32(500000.0) ** (np.arange(half, dtype=np.float32) * np.float32(2.0 / hd)))).astype(np.float32)
        angle = (np.arange(tokens, dtype=np.float32)[:, None] * freq[None, :]).astype(np.float32)
        cos = np.cos(angle.astype(np.float64)).astype(np.float32)
        sin = np.sin(angle.astype(np.float64)).astype(np.float32)
        cos = jnp.asarray(np.concatenate([cos, cos], axis=1))
        sin = jnp.asarray(np.concatenate([-sin, sin], axis=1))
        n_cut = len([1 for _, w in spans(width, ff) for _ in spans(w, 9 * 128)])
        n_chunk = width // KC
        any_spec = pl.BlockSpec(memory_space=pl.ANY)
        vmem = pl.BlockSpec(memory_space=pltpu.VMEM)
        row_buf = pltpu.VMEM((rows, width), BF)
        dma = pltpu.SemaphoreType.DMA
        out, k_cache, v_cache = pl.pallas_call(
            functools.partial(kernel, 1e-5),
            out_shape=(jax.ShapeDtypeStruct((rows, width), BF), jax.ShapeDtypeStruct((tokens, hd), BF),
                       jax.ShapeDtypeStruct((tokens, hd), BF)),
            in_specs=[any_spec] * 12,
            out_specs=(vmem, vmem, vmem),
            scratch_shapes=[
                row_buf, pltpu.VMEM((width // 128, 128), BF), pltpu.VMEM((width // 128, 128), BF),
                pltpu.VMEM((tokens, hd), F32), pltpu.VMEM((tokens, hd), F32),
                pltpu.VMEM((heads, width, hd), BF), pltpu.VMEM((width, 2 * hd), BF),
                pltpu.VMEM((heads * hd, width), BF),
                pltpu.VMEM((N_SLOTS, KC, ff), BF), pltpu.VMEM((tokens, width), BF),
                pltpu.VMEM((tokens, (heads + 2) * hd), F32), pltpu.VMEM((heads * tokens, hd), BF),
                pltpu.VMEM((tokens, heads * hd), BF), pltpu.VMEM((tp_size // 2, rows, width), BF),
                row_buf, row_buf, row_buf, row_buf,
                dma((5,)), dma((width // RAW, 2)), dma(()), dma(()), dma((2 * n_chunk,)), dma((8,)),
                dma((2, n_chunk, 7)), dma((2, n_chunk, 7)), dma((2, n_cut, 4)), dma((2, n_cut, 4)),
            ],
            compiler_params=pltpu.CompilerParams(collective_id=0, has_side_effects=True, vmem_limit_bytes=67_043_328),
        )(hidden_in, attn_norm.reshape(width // 128, 128), mlp_norm.reshape(width // 128, 128), cos, sin,
          jnp.transpose(w_query, (1, 0, 2)), w_key.reshape(width, kv_heads // 2, 2, hd),
          w_value.reshape(width, kv_heads // 2, 2, hd), w_out.reshape(heads * hd, width), w_gate, w_up, w_down)
        results = (out, k_cache, v_cache)
        out, k_cache, v_cache = pl.pallas_call(
            hand_over,
            out_shape=tuple(jax.ShapeDtypeStruct(r.shape, r.dtype) for r in results),
            in_specs=[any_spec] * 3,
            out_specs=(any_spec,) * 3,
            scratch_shapes=[pltpu.VMEM(r.shape, r.dtype) for r in results] + [dma((2, 3))],
        )(*results)
        return out, k_cache.reshape(tokens, 1, hd), v_cache.reshape(tokens, 1, hd)

    row_spec = P(("dp", "tp"), None)
    cache_spec = P("dp", "tp", None)
    return jax.shard_map(local_layer, mesh=mesh, in_specs=(row_spec, P(), P(), P(None, "tp", None), P(), P(), P("tp", None, None), P(None, "tp"), P(None, "tp"), P("tp", None)), out_specs=(row_spec, cache_spec, cache_spec), check_vma=False)
```

time: 81.8 us -> 69.5 us (0.85)
  local copies, waits for them, and re-layouts: 6.98 us -> 0 us
  Pallas kernels: 72.7 us -> 67.5 us
    pallas_call x1, Pallas kernels: 72.7 us -> 65.8 us  [local_layer(): pl.pallas_call(functools.partial(kernel, 1e-05), out_shape=(jax.ShapeDtyp...]
    unnamed x3 -> x0, local copies, waits for them, and re-layouts: 4.34 us -> none
    reshape x2 -> x0, local copies, waits for them, and re-layouts: 2.64 us -> none  [the longest x1 1.32 us: local_layer(): attn_norm.reshape(1, width)]
    pallas_call x0 -> x1, Pallas kernels: none -> 1.65 us  [local_layer(): pl.pallas_call(hand_over, out_shape=tuple((jax.ShapeDtypeStruct(r.shape,...]
where the time goes in v2:
time: 69.5 us; the launch traced here: 68.3 us
  Pallas kernels  67.5 us (97%)
  between operations  0.8 us (1%)
    pallas_call x1, Pallas kernels, local_layer(): pl.pallas_call(functools.partial(kernel, 1e-05), out_shape=(jax.ShapeDtyp...  65.8 us
    pallas_call x1, Pallas kernels, local_layer(): pl.pallas_call(hand_over, out_shape=tuple((jax.ShapeDtypeStruct(r.shape,...  1.65 us

profile of v2, /device:TPU:113, one launch (start us, length us, event | category | flops | bytes accessed | tf_op | source)
XLA Modules:
  0.0 68.3 jit_solution(717693431633252765)
XLA Ops:
  0.6 65.8 %shard_map.139 = (bf16[16,5120]{1,0:T(8,128)(2,1)}, bf16[128,128]{1,0:T(8,128)(2,1)}, bf16[128,128]{1,0:T(8,128)(2,1)}) custom-call(bf16[16,5120]{1,0:T(8,128)(2,1)} %hid_hbm.1, bf16[40,128]{1,0:T(8,128)(2,1)} %bitcast.12, bf16[40,128]{1,0:T(8,128)(2,1)} %bitcast.13, f32[128,128]{1,0:T(8,128)} %constant.4.clone.cos_hbm, f32[128,128]{1,0:T(8,128)} %constant.5.clone.sin_hbm, ...), custom_call_target="tpu_custom_call" | custom-call | tf_op jit(solution)/shard_map/pallas_call | solution.py:390
  66.5 1.6 %shard_map.140 = (bf16[16,5120]{1,0:T(8,128)(2,1)}, bf16[128,128]{1,0:T(8,128)(2,1)}, bf16[128,128]{1,0:T(8,128)(2,1)}) custom-call(bf16[16,5120]{1,0:T(8,128)(2,1)} %get-tuple-element.9.refs_0_, bf16[128,128]{1,0:T(8,128)(2,1)} %get-tuple-element.10.refs_1_, bf16[128,128]{1,0:T(8,128)(2,1)} %get-tuple-element.11.refs_2_), custom_call_target="tpu_custom_call" | custom-call | tf_op jit(solution)/shard_map/pallas_call | solution.py:413
